TPU v7x, 32 devices: a whole 2x2x4 slice. The times are simulated.
32 devices in a mesh: dom: 16 (over z, y, x), sub: 2 (over core).
Axes of the slice: x: 2, y: 2, z: 4, core: 2. Of those that a mesh axis runs over, the one named last changes fastest.
Arguments:
- rhs: float32 [8192], P(('dom', 'sub')), may hold values from -6 to 6
- diagonal: float32 [8192], P(('dom', 'sub')), may hold values from 1 to 2
- self_raw: float32 [8192, 256], P(('dom', 'sub')), may hold values from -0.046875 to 0.046875
- coupling: float32 [8192, 256], P(('dom', 'sub')), may hold values from -0.046875 to 0.046875
- pattern: int32 [64, 2], P(('dom', 'sub')), may hold values 0 or 1
- prolong: float32 [8192, 128], P(('dom', 'sub')), may hold values from -0.5 to 0.5
- coarse_raw: float32 [4096, 256], P('dom'), may hold values from -0.0234375 to 0.0234375
- coarse_diagonal: float32 [4096], P('dom'), may hold values from 1 to 2
Outputs:
- solution: float32 [8192], P(('dom', 'sub'))
- residual: float32 [8192], P(('dom', 'sub'))
- norms: float32 [3], replicated
All inputs are finite; a program needn't handle non-finite values. No bound on the sum of `pattern` on one device may be relied on, other than what follows from the above.
Results may differ from a plain program's by a relative error of at most 0.0003.
Values sent between devices are 32-bit elements; how exact they have to be, the bound alone decides.
No kernel may reach another device: no remote copies, remote signals or barrier semaphores. Data moves between devices by JAX's collectives and lax.ppermute only.
A program may use at most 64 MiB of HBM per device.

v0:
```python
import jax
import jax.numpy as jnp
from jax import lax
from jax.sharding import PartitionSpec as P

ITERS = 3
OMEGA = 0.7
HIGH = lax.Precision.HIGHEST


def passed_along(value, axis, steps):
    count = lax.axis_size(axis)
    initial, last = (max(0, -steps), min(count, count - steps))
    return lax.ppermute(value, axis, [(source, source + steps) for source in range(initial, last)])


def three_sums(resid, uvec, wvec):
    return lax.psum(
        (jnp.sum(resid * uvec), jnp.sum(wvec * uvec), jnp.sum(resid * resid)), ("dom", "sub")
    )


def per_device(rhs, diagonal, self_raw, coupling, pattern, prolong, coarse_raw, coarse_diagonal):
    width = rhs.shape[0]
    blocks = pattern.shape[0]
    block_rows = width // blocks
    coarse = prolong.shape[1]
    eye = jnp.eye(width, dtype=jnp.float32)
    selfm = 0.5 * (self_raw + self_raw.T) * (1.0 - eye) + eye * diagonal[:, None]
    mask = pattern.reshape(blocks, 1, blocks, 1).astype(jnp.float32)
    mask = jnp.broadcast_to(mask, (blocks, block_rows, blocks, block_rows)).reshape(width, width)
    coup = coupling * mask
    dinv = 1.0 / diagonal
    ceye = jnp.eye(2 * coarse, dtype=jnp.float32)
    cmat = 0.5 * (coarse_raw + coarse_raw.T) * (1.0 - ceye) + ceye * coarse_diagonal[:, None]
    cdinv = 1.0 / coarse_diagonal
    offset = lax.axis_index("sub") * coarse

    def apply(vec):
        upper = passed_along(vec, ("dom", "sub"), -1)
        lower = passed_along(jnp.dot(vec, coup, precision=HIGH), ("dom", "sub"), 1)
        return jnp.dot(selfm, vec, precision=HIGH) + jnp.dot(coup, upper, precision=HIGH) + lower

    def precond(wvec):
        first = OMEGA * dinv * wvec
        resid = wvec - apply(first)
        rcoarse = jnp.dot(resid, prolong, precision=HIGH)
        own_inv = lax.dynamic_slice_in_dim(cdinv, offset, coarse, 0)
        own_rows = lax.dynamic_slice_in_dim(cmat, offset, coarse, 0)
        eone = own_inv * rcoarse
        eboth = lax.all_gather(eone, "sub", axis=0, tiled=True)
        mine = eone + own_inv * (rcoarse - jnp.dot(own_rows, eboth, precision=HIGH))
        second = first + jnp.dot(prolong, mine, precision=HIGH)
        return second + OMEGA * dinv * (wvec - apply(second))

    resid = rhs
    solution = jnp.zeros_like(rhs)
    uvec = precond(resid)
    wvec = apply(uvec)
    zeros = jnp.zeros_like(rhs)
    pvec, svec, qvec, zvec = (zeros, zeros, zeros, zeros)
    gamma_prev = jnp.float32(1.0)
    alpha_prev = jnp.float32(1.0)
    norm_list = []
    for step in range(ITERS):
        mvec = precond(wvec)
        nvec = apply(mvec)
        gamma, delta, rnorm = three_sums(resid, uvec, wvec)
        norm_list.append(rnorm)
        if step == 0:
            beta = jnp.float32(0.0)
            alpha = gamma / delta
        else:
            beta = gamma / gamma_prev
            alpha = gamma / (delta - beta * gamma / alpha_prev)
        zvec = nvec + beta * zvec
        qvec = mvec + beta * qvec
        svec = wvec + beta * svec
        pvec = uvec + beta * pvec
        solution = solution + alpha * pvec
        resid = resid - alpha * svec
        uvec = uvec - alpha * qvec
        wvec = wvec - alpha * zvec
        gamma_prev = gamma
        alpha_prev = alpha
    return (solution, resid, jnp.stack(norm_list))


def solution(mesh):
    in_specs = (
        P(("dom", "sub")),
        P(("dom", "sub")),
        P(("dom", "sub"), None),
        P(("dom", "sub"), None),
        P(("dom", "sub"), None),
        P(("dom", "sub"), None),
        P("dom", None),
        P("dom"),
    )
    out_specs = (P(("dom", "sub")), P(("dom", "sub")), P())
    return jax.shard_map(
        per_device, mesh=mesh, in_specs=in_specs, out_specs=out_specs, check_vma=False
    )
```

profile of v0, /device:TPU:0, one launch (start us, length us, event | category | flops | bytes accessed | tf_op | source)
XLA Modules:
  0.0 227.7 jit_solution(16379148000464561736)
XLA Ops:
  0.7 0.8 fusion.22
  1.4 1.3 collective-permute-start
  2.7 0.7 convert_element_type.11
  3.8 3.1 %collective-permute-start.1 = (f32[256]{0:T(256)S(1)}, f32[256]{0:T(256)S(1)}, u32[]{:S(2)}, u32[]{:S(2)}) collective-permute-start(f32[256]{0:T(256)S(1)} %bitcast.255), channel_id=1, source_target_pairs={{0,1},{1,2},{2,3},{3,4},{4,5},{5,6},{6,7},{7,8},{8,9},{9,10},{10,1... | collective-permute-start | bytes 3080 | tf_op jit(solution)/shard_map/ppermute | solution.py:14
  8.0 0.7 copy-done.2
  8.8 0.7 copy-done.6
  10.0 0.7 copy-done.4
  10.9 4.0 %all-gather = f32[2,1,128]{2,1,0:T(1,128)S(1)} all-gather(f32[1,1,128]{2,1,0:T(1,128)S(1)} %bitcast.253), channel_id=1, replica_groups=mesh['dom'=16,'sub'=2] {'sub'}, dimensions={0}, use_global_device_ids=true | all-gather | bytes 1536 | tf_op jit(solution)/shard_map/all_gather | solution.py:51
  15.4 1.3 collective-permute-start.2
  17.2 3.1 %collective-permute-start.3 = (f32[256]{0:T(256)S(1)}, f32[256]{0:T(256)S(1)}, u32[]{:S(2)}, u32[]{:S(2)}) collective-permute-start(f32[256]{0:T(256)S(1)} %bitcast.263), channel_id=1, source_target_pairs={{0,1},{1,2},{2,3},{3,4},{4,5},{5,6},{6,7},{7,8},{8,9},{9,10},{10,1... | collective-permute-start | bytes 3080 | tf_op jit(solution)/shard_map/ppermute | solution.py:14
  21.1 1.3 collective-permute-start.4
  22.9 4.5 %collective-permute-start.5 = (f32[256]{0:T(256)S(1)}, f32[256]{0:T(256)S(1)}, u32[]{:S(2)}, u32[]{:S(2)}) collective-permute-start(f32[256]{0:T(256)S(1)} %bitcast.265), channel_id=1, source_target_pairs={{0,1},{1,2},{2,3},{3,4},{4,5},{5,6},{6,7},{7,8},{8,9},{9,10},{10,1... | collective-permute-start | bytes 3080 | tf_op jit(solution)/shard_map/ppermute | solution.py:14
  28.2 1.3 collective-permute-start.6
  30.0 4.8 %collective-permute-start.7 = (f32[256]{0:T(256)S(1)}, f32[256]{0:T(256)S(1)}, u32[]{:S(2)}, u32[]{:S(2)}) collective-permute-start(f32[256]{0:T(256)S(1)} %bitcast.267), channel_id=1, source_target_pairs={{0,1},{1,2},{2,3},{3,4},{4,5},{5,6},{6,7},{7,8},{8,9},{9,10},{10,1... | collective-permute-start | bytes 3080 | tf_op jit(solution)/shard_map/ppermute | solution.py:14
  35.7 3.6 %all-gather.1 = f32[2,1,128]{2,1,0:T(1,128)S(1)} all-gather(f32[1,1,128]{2,1,0:T(1,128)S(1)} %bitcast.252), channel_id=1, replica_groups=mesh['dom'=16,'sub'=2] {'sub'}, dimensions={0}, use_global_device_ids=true | all-gather | bytes 1536 | tf_op jit(solution)/shard_map/all_gather | solution.py:51
  39.8 1.3 collective-permute-start.8
  41.6 3.1 %collective-permute-start.9 = (f32[256]{0:T(256)S(1)}, f32[256]{0:T(256)S(1)}, u32[]{:S(2)}, u32[]{:S(2)}) collective-permute-start(f32[256]{0:T(256)S(1)} %bitcast.269), channel_id=1, source_target_pairs={{0,1},{1,2},{2,3},{3,4},{4,5},{5,6},{6,7},{7,8},{8,9},{9,10},{10,1... | collective-permute-start | bytes 3080 | tf_op jit(solution)/shard_map/ppermute | solution.py:14
  46.1 1.3 collective-permute-start.10
  47.9 6.8 %collective-permute-start.11 = (f32[256]{0:T(256)S(1)}, f32[256]{0:T(256)S(1)}, u32[]{:S(2)}, u32[]{:S(2)}) collective-permute-start(f32[256]{0:T(256)S(1)} %bitcast.259), channel_id=1, source_target_pairs={{0,1},{1,2},{2,3},{3,4},{4,5},{5,6},{6,7},{7,8},{8,9},{9,10},{10,1... | collective-permute-start | bytes 3080 | tf_op jit(solution)/shard_map/ppermute | solution.py:14
  54.7 49.2 %all-reduce.2 = (f32[]{:T(128)}, f32[]{:T(128)}) all-reduce(f32[]{:T(128)} %get-tuple-element.7, f32[]{:T(128)} %get-tuple-element.8), channel_id=1, replica_groups=mesh['dom'=16,'sub'=2] {'dom','sub'}, use_global_device_ids=true, to_apply=%region_1.0 | all-reduce | flops 2 | bytes 16 | tf_op jit(solution)/shard_map/psum | solution.py:18
  105.5 0.7 multiply_reduce_fusion.5
  106.2 1.3 collective-permute-start.12
  108.0 41.2 %all-reduce.1 = (f32[]{:T(128)}, f32[]{:T(128)}) all-reduce(f32[]{:T(128)} %get-tuple-element.4, f32[]{:T(128)} %get-tuple-element.3), channel_id=1, replica_groups=mesh['dom'=16,'sub'=2] {'dom','sub'}, use_global_device_ids=true, to_apply=%region_5.0 | all-reduce | flops 2 | bytes 16 | tf_op jit(solution)/shard_map/psum | solution.py:18
  150.6 1.3 collective-permute-start.13
  155.6 4.5 %all-gather.2 = f32[2,1,128]{2,1,0:T(1,128)S(1)} all-gather(f32[1,1,128]{2,1,0:T(1,128)S(1)} %bitcast.251), channel_id=1, replica_groups=mesh['dom'=16,'sub'=2] {'sub'}, dimensions={0}, use_global_device_ids=true | all-gather | bytes 1536 | tf_op jit(solution)/shard_map/all_gather | solution.py:51
  160.5 1.3 collective-permute-start.14
  162.3 3.1 %collective-permute-start.15 = (f32[256]{0:T(256)S(1)}, f32[256]{0:T(256)S(1)}, u32[]{:S(2)}, u32[]{:S(2)}) collective-permute-start(f32[256]{0:T(256)S(1)} %bitcast.271), channel_id=1, source_target_pairs={{0,1},{1,2},{2,3},{3,4},{4,5},{5,6},{6,7},{7,8},{8,9},{9,10},{10,1... | collective-permute-start | bytes 3080 | tf_op jit(solution)/shard_map/ppermute | solution.py:14
  166.2 1.3 collective-permute-start.16
  168.0 4.1 %collective-permute-start.17 = (f32[256]{0:T(256)S(1)}, f32[256]{0:T(256)S(1)}, u32[]{:S(2)}, u32[]{:S(2)}) collective-permute-start(f32[256]{0:T(256)S(1)} %bitcast.261), channel_id=1, source_target_pairs={{0,1},{1,2},{2,3},{3,4},{4,5},{5,6},{6,7},{7,8},{8,9},{9,10},{10,1... | collective-permute-start | bytes 3080 | tf_op jit(solution)/shard_map/ppermute | solution.py:14
  172.8 0.7 multiply_reduce_fusion
  173.5 47.3 %all-reduce = (f32[]{:T(128)}, f32[]{:T(128)}, f32[1]{0:T(128)}, f32[1]{0:T(128)}, f32[1]{0:T(128)}) all-reduce(f32[]{:T(128)} %get-tuple-element.10, f32[]{:T(128)} %get-tuple-element.11, f32[1]{0:T(128)} %bitcast.82, f32[1]{0:T(128)} %bitcast.81, f32[1]{0:T(128)} %bitcast.80), channel_id=1, replica_groups=mesh['dom'=16,'sub'=2] {'dom','sub'}, use_global_device_ids=true, to_apply=%region_9.0 | all-reduce | flops 5 | bytes 40 | tf_op jit(solution)/shard_map/psum | solution.py:18
  224.7 2.4 %pad_maximum_fusion = f32[3]{0:T(128)} fusion(f32[1]{0:T(128)} %get-tuple-element.14, f32[1]{0:T(128)} %get-tuple-element.15, f32[1]{0:T(128)} %get-tuple-element.16), kind=kLoop, calls=%fused_computation.59 | loop fusion | flops 6 | bytes 24 | tf_op jit(solution)/shard_map/stack | solution.py:86
  (88 shorter events, 14.5 us)
Async XLA Ops:
  0.6 10.1 %copy-start = (f32[256,128]{1,0:T(8,128)S(1)}, f32[256,128]{1,0:T(8,128)}, u32[]{:S(2)}) copy-start(f32[256,128]{1,0:T(8,128)} %param.13) | copy-start | bytes 393220
  0.6 2.9 %copy-start.3 = (f32[256,256]{1,0:T(8,128)S(1)}, f32[256,256]{1,0:T(8,128)}, u32[]{:S(2)}) copy-start(f32[256,256]{1,0:T(8,128)} %param.11) | copy-start | bytes 786436
  1.4 8.3 %collective-permute-start = (f32[256]{0:T(256)S(1)}, f32[256]{0:T(256)S(1)}, u32[]{:S(2)}, u32[]{:S(2)}) collective-permute-start(f32[256]{0:T(256)S(1)} %get-tuple-element.30), channel_id=1, source_target_pairs={{1,0},{2,1},{3,2},{4,3},{5,4},{6,5},{7,6},{8,7},{9,8},{10,9},{11,1... | collective-permute-start | bytes 3080 | tf_op jit(solution)/shard_map/ppermute | solution.py:14
  3.6 3.3 %copy-start.1 = (f32[256,256]{1,0:T(8,128)S(1)}, f32[256,256]{1,0:T(8,128)}, u32[]{:S(2)}) copy-start(f32[256,256]{1,0:T(8,128)} %param.10) | copy-start | bytes 786436
  3.8 6.2 %collective-permute-start.1 = (f32[256]{0:T(256)S(1)}, f32[256]{0:T(256)S(1)}, u32[]{:S(2)}, u32[]{:S(2)}) collective-permute-start(f32[256]{0:T(256)S(1)} %bitcast.255), channel_id=1, source_target_pairs={{0,1},{1,2},{2,3},{3,4},{4,5},{5,6},{6,7},{7,8},{8,9},{9,10},{10,1... | collective-permute-start | bytes 3080 | tf_op jit(solution)/shard_map/ppermute | solution.py:14
  6.9 0.7 copy-start.5
  7.7 1.0 copy-start.2
  8.8 0.7 copy-start.6
  9.9 0.7 copy-start.4
  15.4 4.9 %collective-permute-start.2 = (f32[256]{0:T(256)S(1)}, f32[256]{0:T(256)S(1)}, u32[]{:S(2)}, u32[]{:S(2)}) collective-permute-start(f32[256]{0:T(256)S(1)} %add.151), channel_id=1, source_target_pairs={{1,0},{2,1},{3,2},{4,3},{5,4},{6,5},{7,6},{8,7},{9,8},{10,9},{11,1... | collective-permute-start | bytes 3080 | tf_op jit(solution)/shard_map/ppermute | solution.py:14
  17.2 3.9 %collective-permute-start.3 = (f32[256]{0:T(256)S(1)}, f32[256]{0:T(256)S(1)}, u32[]{:S(2)}, u32[]{:S(2)}) collective-permute-start(f32[256]{0:T(256)S(1)} %bitcast.263), channel_id=1, source_target_pairs={{0,1},{1,2},{2,3},{3,4},{4,5},{5,6},{6,7},{7,8},{8,9},{9,10},{10,1... | collective-permute-start | bytes 3080 | tf_op jit(solution)/shard_map/ppermute | solution.py:14
  21.1 6.3 %collective-permute-start.4 = (f32[256]{0:T(256)S(1)}, f32[256]{0:T(256)S(1)}, u32[]{:S(2)}, u32[]{:S(2)}) collective-permute-start(f32[256]{0:T(256)S(1)} %multiply_add_fusion.4), channel_id=1, source_target_pairs={{1,0},{2,1},{3,2},{4,3},{5,4},{6,5},{7,6},{8,7},{9,8},{10,9},{11,1... | collective-permute-start | bytes 3080 | tf_op jit(solution)/shard_map/ppermute | solution.py:14
  22.9 5.3 %collective-permute-start.5 = (f32[256]{0:T(256)S(1)}, f32[256]{0:T(256)S(1)}, u32[]{:S(2)}, u32[]{:S(2)}) collective-permute-start(f32[256]{0:T(256)S(1)} %bitcast.265), channel_id=1, source_target_pairs={{0,1},{1,2},{2,3},{3,4},{4,5},{5,6},{6,7},{7,8},{8,9},{9,10},{10,1... | collective-permute-start | bytes 3080 | tf_op jit(solution)/shard_map/ppermute | solution.py:14
  28.2 6.6 %collective-permute-start.6 = (f32[256]{0:T(256)S(1)}, f32[256]{0:T(256)S(1)}, u32[]{:S(2)}, u32[]{:S(2)}) collective-permute-start(f32[256]{0:T(256)S(1)} %get-tuple-element.26), channel_id=1, source_target_pairs={{1,0},{2,1},{3,2},{4,3},{5,4},{6,5},{7,6},{8,7},{9,8},{10,9},{11,1... | collective-permute-start | bytes 3080 | tf_op jit(solution)/shard_map/ppermute | solution.py:14
  30.0 5.6 %collective-permute-start.7 = (f32[256]{0:T(256)S(1)}, f32[256]{0:T(256)S(1)}, u32[]{:S(2)}, u32[]{:S(2)}) collective-permute-start(f32[256]{0:T(256)S(1)} %bitcast.267), channel_id=1, source_target_pairs={{0,1},{1,2},{2,3},{3,4},{4,5},{5,6},{6,7},{7,8},{8,9},{9,10},{10,1... | collective-permute-start | bytes 3080 | tf_op jit(solution)/shard_map/ppermute | solution.py:14
  39.8 4.9 %collective-permute-start.8 = (f32[256]{0:T(256)S(1)}, f32[256]{0:T(256)S(1)}, u32[]{:S(2)}, u32[]{:S(2)}) collective-permute-start(f32[256]{0:T(256)S(1)} %add.160), channel_id=1, source_target_pairs={{1,0},{2,1},{3,2},{4,3},{5,4},{6,5},{7,6},{8,7},{9,8},{10,9},{11,1... | collective-permute-start | bytes 3080 | tf_op jit(solution)/shard_map/ppermute | solution.py:14
  41.6 3.9 %collective-permute-start.9 = (f32[256]{0:T(256)S(1)}, f32[256]{0:T(256)S(1)}, u32[]{:S(2)}, u32[]{:S(2)}) collective-permute-start(f32[256]{0:T(256)S(1)} %bitcast.269), channel_id=1, source_target_pairs={{0,1},{1,2},{2,3},{3,4},{4,5},{5,6},{6,7},{7,8},{8,9},{9,10},{10,1... | collective-permute-start | bytes 3080 | tf_op jit(solution)/shard_map/ppermute | solution.py:14
  46.1 59.1 %collective-permute-start.10 = (f32[256]{0:T(256)S(1)}, f32[256]{0:T(256)S(1)}, u32[]{:S(2)}, u32[]{:S(2)}) collective-permute-start(f32[256]{0:T(256)S(1)} %get-tuple-element.32), channel_id=1, source_target_pairs={{1,0},{2,1},{3,2},{4,3},{5,4},{6,5},{7,6},{8,7},{9,8},{10,9},{11,1... | collective-permute-start | bytes 3080 | tf_op jit(solution)/shard_map/ppermute | solution.py:14
  47.9 57.6 %collective-permute-start.11 = (f32[256]{0:T(256)S(1)}, f32[256]{0:T(256)S(1)}, u32[]{:S(2)}, u32[]{:S(2)}) collective-permute-start(f32[256]{0:T(256)S(1)} %bitcast.259), channel_id=1, source_target_pairs={{0,1},{1,2},{2,3},{3,4},{4,5},{5,6},{6,7},{7,8},{8,9},{9,10},{10,1... | collective-permute-start | bytes 3080 | tf_op jit(solution)/shard_map/ppermute | solution.py:14
  106.2 48.8 %collective-permute-start.12 = (f32[256]{0:T(256)S(1)}, f32[256]{0:T(256)S(1)}, u32[]{:S(2)}, u32[]{:S(2)}) collective-permute-start(f32[256]{0:T(256)S(1)} %mul.220), channel_id=1, source_target_pairs={{1,0},{2,1},{3,2},{4,3},{5,4},{6,5},{7,6},{8,7},{9,8},{10,9},{11,1... | collective-permute-start | bytes 3080 | tf_op jit(solution)/shard_map/ppermute | solution.py:14
  150.6 4.7 %collective-permute-start.13 = (f32[256]{0:T(256)S(1)}, f32[256]{0:T(256)S(1)}, u32[]{:S(2)}, u32[]{:S(2)}) collective-permute-start(f32[256]{0:T(256)S(1)} %bitcast.257), channel_id=1, source_target_pairs={{0,1},{1,2},{2,3},{3,4},{4,5},{5,6},{6,7},{7,8},{8,9},{9,10},{10,1... | collective-permute-start | bytes 3080 | tf_op jit(solution)/shard_map/ppermute | solution.py:14
  160.5 4.9 %collective-permute-start.14 = (f32[256]{0:T(256)S(1)}, f32[256]{0:T(256)S(1)}, u32[]{:S(2)}, u32[]{:S(2)}) collective-permute-start(f32[256]{0:T(256)S(1)} %add.172), channel_id=1, source_target_pairs={{1,0},{2,1},{3,2},{4,3},{5,4},{6,5},{7,6},{8,7},{9,8},{10,9},{11,1... | collective-permute-start | bytes 3080 | tf_op jit(solution)/shard_map/ppermute | solution.py:14
  162.3 3.9 %collective-permute-start.15 = (f32[256]{0:T(256)S(1)}, f32[256]{0:T(256)S(1)}, u32[]{:S(2)}, u32[]{:S(2)}) collective-permute-start(f32[256]{0:T(256)S(1)} %bitcast.271), channel_id=1, source_target_pairs={{0,1},{1,2},{2,3},{3,4},{4,5},{5,6},{6,7},{7,8},{8,9},{9,10},{10,1... | collective-permute-start | bytes 3080 | tf_op jit(solution)/shard_map/ppermute | solution.py:14
  166.2 5.9 %collective-permute-start.16 = (f32[256]{0:T(256)S(1)}, f32[256]{0:T(256)S(1)}, u32[]{:S(2)}, u32[]{:S(2)}) collective-permute-start(f32[256]{0:T(256)S(1)} %multiply_add_fusion.1), channel_id=1, source_target_pairs={{1,0},{2,1},{3,2},{4,3},{5,4},{6,5},{7,6},{8,7},{9,8},{10,9},{11,1... | collective-permute-start | bytes 3080 | tf_op jit(solution)/shard_map/ppermute | solution.py:14
  168.0 4.9 %collective-permute-start.17 = (f32[256]{0:T(256)S(1)}, f32[256]{0:T(256)S(1)}, u32[]{:S(2)}, u32[]{:S(2)}) collective-permute-start(f32[256]{0:T(256)S(1)} %bitcast.261), channel_id=1, source_target_pairs={{0,1},{1,2},{2,3},{3,4},{4,5},{5,6},{6,7},{7,8},{8,9},{9,10},{10,1... | collective-permute-start | bytes 3080 | tf_op jit(solution)/shard_map/ppermute | solution.py:14
where the time goes:
time: 229 us; the launch traced here: 228 us
  blocking collectives  150 us (66%)
  starting transfers between devices  45.3 us (20%)
  between operations  10.8 us (5%)
  matrix products  8.57 us (4%)
  other arithmetic  6.91 us (3%)
  waiting for transfers between devices  3.15 us (1%)
  local copies, waits for them, and re-layouts  3.1 us (1%)
    psum x3, blocking collectives, three_sums(): lax.psum((jnp.sum(resid * uvec), jnp.sum(wvec * uvec), jnp.sum(resid * re...  138 us
    ppermute x18, starting transfers between devices, passed_along(): lax.ppermute(value, axis, [(source, source + steps) for source in range(i...  45.3 us
    all_gather x3, blocking collectives, precond(): eboth = lax.all_gather(eone, 'sub', axis=0, tiled=True)  12.2 us
  transfers between devices with their start and end apart: 18, of which 6 were waited for; matrix products, arithmetic and copies ran while one was open for 4% of the time, Pallas kernels for 0%

commit v1 on v0

--- a/solution.py
+++ b/solution.py
@@ -16,7 +16,8 @@
 
 def three_sums(resid, uvec, wvec):
     return lax.psum(
-        (jnp.sum(resid * uvec), jnp.sum(wvec * uvec), jnp.sum(resid * resid)), ("dom", "sub")
+        lax.psum((jnp.sum(resid * uvec), jnp.sum(wvec * uvec), jnp.sum(resid * resid)), "dom"),
+        "sub",
     )
 
 

time: 229 us -> 227 us (level)
  blocking collectives: 150 us -> 147 us
    psum x3, blocking collectives: 138 us -> 128 us  [three_sums(): lax.psum((jnp.sum(resid * uvec), jnp.sum(wvec * uvec), jnp.sum(resid * re...]
    psum x0 -> x3, blocking collectives: none -> 9.36 us  [three_sums(): lax.psum(lax.psum((jnp.sum(resid * uvec), jnp.sum(wvec * uvec), jnp.sum(r...]
    all_gather x3, blocking collectives: 12.2 us -> 9.5 us  [precond(): eboth = lax.all_gather(eone, 'sub', axis=0, tiled=True)]
where the time goes in v1:
time: 227 us; the launch traced here: 226 us
  blocking collectives  147 us (65%)
  starting transfers between devices  45.9 us (20%)
  between operations  11.1 us (5%)
  matrix products  8.57 us (4%)
  other arithmetic  6.95 us (3%)
  waiting for transfers between devices  3.15 us (1%)
  local copies, waits for them, and re-layouts  3.1 us (1%)
    psum x3, blocking collectives, three_sums(): lax.psum((jnp.sum(resid * uvec), jnp.sum(wvec * uvec), jnp.sum(resid * re...  128 us
    ppermute x18, starting transfers between devices, passed_along(): lax.ppermute(value, axis, [(source, source + steps) for source in range(i...  45.9 us
    all_gather x3, blocking collectives, precond(): eboth = lax.all_gather(eone, 'sub', axis=0, tiled=True)  9.5 us
    psum x3, blocking collectives, three_sums(): lax.psum(lax.psum((jnp.sum(resid * uvec), jnp.sum(wvec * uvec), jnp.sum(r...  9.36 us
  transfers between devices with their start and end apart: 18, of which 6 were waited for; matrix products, arithmetic and copies ran while one was open for 4% of the time, Pallas kernels for 0%

profile of v1, /device:TPU:0, one launch (start us, length us, event | category | flops | bytes accessed | tf_op | source)
XLA Modules:
  0.0 225.7 jit_solution(18311400962732765076)
XLA Ops:
  0.7 0.8 fusion.22
  1.4 1.3 collective-permute-start
  2.7 0.7 convert_element_type.11
  3.8 3.1 %collective-permute-start.1 = (f32[256]{0:T(256)S(1)}, f32[256]{0:T(256)S(1)}, u32[]{:S(2)}, u32[]{:S(2)}) collective-permute-start(f32[256]{0:T(256)S(1)} %bitcast.255), channel_id=1, source_target_pairs={{0,1},{1,2},{2,3},{3,4},{4,5},{5,6},{6,7},{7,8},{8,9},{9,10},{10,1... | collective-permute-start | bytes 3080 | tf_op jit(solution)/shard_map/ppermute | solution.py:14
  10.0 0.7 copy-done.4
  10.9 4.0 %all-gather = f32[2,1,128]{2,1,0:T(1,128)S(1)} all-gather(f32[1,1,128]{2,1,0:T(1,128)S(1)} %bitcast.253), channel_id=1, replica_groups=mesh['dom'=16,'sub'=2] {'sub'}, dimensions={0}, use_global_device_ids=true | all-gather | bytes 1536 | tf_op jit(solution)/shard_map/all_gather | solution.py:52
  15.4 1.3 collective-permute-start.2
  17.2 3.1 %collective-permute-start.3 = (f32[256]{0:T(256)S(1)}, f32[256]{0:T(256)S(1)}, u32[]{:S(2)}, u32[]{:S(2)}) collective-permute-start(f32[256]{0:T(256)S(1)} %bitcast.263), channel_id=1, source_target_pairs={{0,1},{1,2},{2,3},{3,4},{4,5},{5,6},{6,7},{7,8},{8,9},{9,10},{10,1... | collective-permute-start | bytes 3080 | tf_op jit(solution)/shard_map/ppermute | solution.py:14
  21.1 1.3 collective-permute-start.4
  22.9 4.5 %collective-permute-start.5 = (f32[256]{0:T(256)S(1)}, f32[256]{0:T(256)S(1)}, u32[]{:S(2)}, u32[]{:S(2)}) collective-permute-start(f32[256]{0:T(256)S(1)} %bitcast.265), channel_id=1, source_target_pairs={{0,1},{1,2},{2,3},{3,4},{4,5},{5,6},{6,7},{7,8},{8,9},{9,10},{10,1... | collective-permute-start | bytes 3080 | tf_op jit(solution)/shard_map/ppermute | solution.py:14
  28.2 1.3 collective-permute-start.6
  30.0 4.8 %collective-permute-start.7 = (f32[256]{0:T(256)S(1)}, f32[256]{0:T(256)S(1)}, u32[]{:S(2)}, u32[]{:S(2)}) collective-permute-start(f32[256]{0:T(256)S(1)} %bitcast.267), channel_id=1, source_target_pairs={{0,1},{1,2},{2,3},{3,4},{4,5},{5,6},{6,7},{7,8},{8,9},{9,10},{10,1... | collective-permute-start | bytes 3080 | tf_op jit(solution)/shard_map/ppermute | solution.py:14
  35.7 3.6 %all-gather.1 = f32[2,1,128]{2,1,0:T(1,128)S(1)} all-gather(f32[1,1,128]{2,1,0:T(1,128)S(1)} %bitcast.252), channel_id=1, replica_groups=mesh['dom'=16,'sub'=2] {'sub'}, dimensions={0}, use_global_device_ids=true | all-gather | bytes 1536 | tf_op jit(solution)/shard_map/all_gather | solution.py:52
  39.8 1.3 collective-permute-start.8
  41.6 3.1 %collective-permute-start.9 = (f32[256]{0:T(256)S(1)}, f32[256]{0:T(256)S(1)}, u32[]{:S(2)}, u32[]{:S(2)}) collective-permute-start(f32[256]{0:T(256)S(1)} %bitcast.269), channel_id=1, source_target_pairs={{0,1},{1,2},{2,3},{3,4},{4,5},{5,6},{6,7},{7,8},{8,9},{9,10},{10,1... | collective-permute-start | bytes 3080 | tf_op jit(solution)/shard_map/ppermute | solution.py:14
  46.1 1.3 collective-permute-start.10
  47.9 6.8 %collective-permute-start.11 = (f32[256]{0:T(256)S(1)}, f32[256]{0:T(256)S(1)}, u32[]{:S(2)}, u32[]{:S(2)}) collective-permute-start(f32[256]{0:T(256)S(1)} %bitcast.259), channel_id=1, source_target_pairs={{0,1},{1,2},{2,3},{3,4},{4,5},{5,6},{6,7},{7,8},{8,9},{9,10},{10,1... | collective-permute-start | bytes 3080 | tf_op jit(solution)/shard_map/ppermute | solution.py:14
  54.7 46.9 %all-reduce.2 = (f32[]{:T(128)}, f32[]{:T(128)}) all-reduce(f32[]{:T(128)} %get-tuple-element.7, f32[]{:T(128)} %get-tuple-element.8), channel_id=1, replica_groups=mesh['dom'=16,'sub'=2] {'dom'}, use_global_device_ids=true, to_apply=%region_1.0 | all-reduce | flops 2 | bytes 16 | tf_op jit(solution)/shard_map/psum | solution.py:19
  101.6 3.1 %all-reduce.5 = (f32[]{:T(128)}, f32[]{:T(128)}) all-reduce(f32[]{:T(128)} %get-tuple-element.19, f32[]{:T(128)} %get-tuple-element.20), channel_id=1, replica_groups=mesh['dom'=16,'sub'=2] {'sub'}, use_global_device_ids=true, to_apply=%region_2.0 | all-reduce | flops 2 | bytes 16 | tf_op jit(solution)/shard_map/psum | solution.py:18
  106.3 0.7 multiply_reduce_fusion.5
  107.0 1.3 collective-permute-start.12
  108.8 39.6 %all-reduce.1 = (f32[]{:T(128)}, f32[]{:T(128)}) all-reduce(f32[]{:T(128)} %get-tuple-element.4, f32[]{:T(128)} %get-tuple-element.3), channel_id=1, replica_groups=mesh['dom'=16,'sub'=2] {'dom'}, use_global_device_ids=true, to_apply=%region_7.0 | all-reduce | flops 2 | bytes 16 | tf_op jit(solution)/shard_map/psum | solution.py:19
  148.4 3.2 %all-reduce.4 = (f32[]{:T(128)}, f32[]{:T(128)}) all-reduce(f32[]{:T(128)} %get-tuple-element.17, f32[]{:T(128)} %get-tuple-element.18), channel_id=1, replica_groups=mesh['dom'=16,'sub'=2] {'sub'}, use_global_device_ids=true, to_apply=%region_8.0 | all-reduce | flops 2 | bytes 16 | tf_op jit(solution)/shard_map/psum | solution.py:18
  152.9 2.1 collective-permute-start.13
  158.9 1.8 all-gather.2
  161.1 1.3 collective-permute-start.14
  162.9 3.1 %collective-permute-start.15 = (f32[256]{0:T(256)S(1)}, f32[256]{0:T(256)S(1)}, u32[]{:S(2)}, u32[]{:S(2)}) collective-permute-start(f32[256]{0:T(256)S(1)} %bitcast.271), channel_id=1, source_target_pairs={{0,1},{1,2},{2,3},{3,4},{4,5},{5,6},{6,7},{7,8},{8,9},{9,10},{10,1... | collective-permute-start | bytes 3080 | tf_op jit(solution)/shard_map/ppermute | solution.py:14
  166.8 1.3 collective-permute-start.16
  168.6 3.9 %collective-permute-start.17 = (f32[256]{0:T(256)S(1)}, f32[256]{0:T(256)S(1)}, u32[]{:S(2)}, u32[]{:S(2)}) collective-permute-start(f32[256]{0:T(256)S(1)} %bitcast.261), channel_id=1, source_target_pairs={{0,1},{1,2},{2,3},{3,4},{4,5},{5,6},{6,7},{7,8},{8,9},{9,10},{10,1... | collective-permute-start | bytes 3080 | tf_op jit(solution)/shard_map/ppermute | solution.py:14
  173.9 41.6 %all-reduce = (f32[]{:T(128)}, f32[]{:T(128)}, f32[]{:T(128)}, f32[]{:T(128)}, f32[]{:T(128)}) all-reduce(f32[]{:T(128)} %get-tuple-element.10, f32[]{:T(128)} %get-tuple-element.11, f32[]{:T(128)} %get-tuple-element.9, f32[]{:T(128)} %get-tuple-element.5, f32[]{:T(128)} %get-tuple-element.6), channel_id=1, replica_groups=mesh['dom'=16,'sub'=2] {'dom'}, use_global_device_ids=true, to_apply=%region_13.0 | all-reduce | flops 5 | bytes 40 | tf_op jit(solution)/shard_map/psum | solution.py:19
  215.5 3.1 %all-reduce.3 = (f32[]{:T(128)}, f32[]{:T(128)}, f32[1]{0:T(128)}, f32[1]{0:T(128)}, f32[1]{0:T(128)}) all-reduce(f32[]{:T(128)} %get-tuple-element.12, f32[]{:T(128)} %get-tuple-element.13, f32[1]{0:T(128)} %bitcast.82, f32[1]{0:T(128)} %bitcast.81, f32[1]{0:T(128)} %bitcast.80), channel_id=1, replica_groups=mesh['dom'=16,'sub'=2] {'sub'}, use_global_device_ids=true, to_apply=%region_14.0 | all-reduce | flops 5 | bytes 40 | tf_op jit(solution)/shard_map/psum | solution.py:18
  222.6 2.5 %pad_maximum_fusion = f32[3]{0:T(128)} fusion(f32[1]{0:T(128)} %get-tuple-element.23, f32[1]{0:T(128)} %get-tuple-element.24, f32[1]{0:T(128)} %get-tuple-element.25), kind=kLoop, calls=%fused_computation.59 | loop fusion | flops 6 | bytes 24 | tf_op jit(solution)/shard_map/stack | solution.py:87
  (91 shorter events, 16.5 us)
Async XLA Ops:
  0.6 10.1 %copy-start = (f32[256,128]{1,0:T(8,128)S(1)}, f32[256,128]{1,0:T(8,128)}, u32[]{:S(2)}) copy-start(f32[256,128]{1,0:T(8,128)} %param.13) | copy-start | bytes 393220
  0.6 2.9 %copy-start.3 = (f32[256,256]{1,0:T(8,128)S(1)}, f32[256,256]{1,0:T(8,128)}, u32[]{:S(2)}) copy-start(f32[256,256]{1,0:T(8,128)} %param.11) | copy-start | bytes 786436
  1.4 8.3 %collective-permute-start = (f32[256]{0:T(256)S(1)}, f32[256]{0:T(256)S(1)}, u32[]{:S(2)}, u32[]{:S(2)}) collective-permute-start(f32[256]{0:T(256)S(1)} %get-tuple-element.39), channel_id=1, source_target_pairs={{1,0},{2,1},{3,2},{4,3},{5,4},{6,5},{7,6},{8,7},{9,8},{10,9},{11,1... | collective-permute-start | bytes 3080 | tf_op jit(solution)/shard_map/ppermute | solution.py:14
  3.6 3.3 %copy-start.1 = (f32[256,256]{1,0:T(8,128)S(1)}, f32[256,256]{1,0:T(8,128)}, u32[]{:S(2)}) copy-start(f32[256,256]{1,0:T(8,128)} %param.10) | copy-start | bytes 786436
  3.8 6.2 %collective-permute-start.1 = (f32[256]{0:T(256)S(1)}, f32[256]{0:T(256)S(1)}, u32[]{:S(2)}, u32[]{:S(2)}) collective-permute-start(f32[256]{0:T(256)S(1)} %bitcast.255), channel_id=1, source_target_pairs={{0,1},{1,2},{2,3},{3,4},{4,5},{5,6},{6,7},{7,8},{8,9},{9,10},{10,1... | collective-permute-start | bytes 3080 | tf_op jit(solution)/shard_map/ppermute | solution.py:14
  6.9 0.7 copy-start.5
  7.7 1.0 copy-start.2
  8.8 0.7 copy-start.6
  9.9 0.7 copy-start.4
  15.4 4.9 %collective-permute-start.2 = (f32[256]{0:T(256)S(1)}, f32[256]{0:T(256)S(1)}, u32[]{:S(2)}, u32[]{:S(2)}) collective-permute-start(f32[256]{0:T(256)S(1)} %add.169), channel_id=1, source_target_pairs={{1,0},{2,1},{3,2},{4,3},{5,4},{6,5},{7,6},{8,7},{9,8},{10,9},{11,1... | collective-permute-start | bytes 3080 | tf_op jit(solution)/shard_map/ppermute | solution.py:14
  17.2 3.9 %collective-permute-start.3 = (f32[256]{0:T(256)S(1)}, f32[256]{0:T(256)S(1)}, u32[]{:S(2)}, u32[]{:S(2)}) collective-permute-start(f32[256]{0:T(256)S(1)} %bitcast.263), channel_id=1, source_target_pairs={{0,1},{1,2},{2,3},{3,4},{4,5},{5,6},{6,7},{7,8},{8,9},{9,10},{10,1... | collective-permute-start | bytes 3080 | tf_op jit(solution)/shard_map/ppermute | solution.py:14
  21.1 6.3 %collective-permute-start.4 = (f32[256]{0:T(256)S(1)}, f32[256]{0:T(256)S(1)}, u32[]{:S(2)}, u32[]{:S(2)}) collective-permute-start(f32[256]{0:T(256)S(1)} %multiply_add_fusion.4), channel_id=1, source_target_pairs={{1,0},{2,1},{3,2},{4,3},{5,4},{6,5},{7,6},{8,7},{9,8},{10,9},{11,1... | collective-permute-start | bytes 3080 | tf_op jit(solution)/shard_map/ppermute | solution.py:14
  22.9 5.3 %collective-permute-start.5 = (f32[256]{0:T(256)S(1)}, f32[256]{0:T(256)S(1)}, u32[]{:S(2)}, u32[]{:S(2)}) collective-permute-start(f32[256]{0:T(256)S(1)} %bitcast.265), channel_id=1, source_target_pairs={{0,1},{1,2},{2,3},{3,4},{4,5},{5,6},{6,7},{7,8},{8,9},{9,10},{10,1... | collective-permute-start | bytes 3080 | tf_op jit(solution)/shard_map/ppermute | solution.py:14
  28.2 6.6 %collective-permute-start.6 = (f32[256]{0:T(256)S(1)}, f32[256]{0:T(256)S(1)}, u32[]{:S(2)}, u32[]{:S(2)}) collective-permute-start(f32[256]{0:T(256)S(1)} %get-tuple-element.35), channel_id=1, source_target_pairs={{1,0},{2,1},{3,2},{4,3},{5,4},{6,5},{7,6},{8,7},{9,8},{10,9},{11,1... | collective-permute-start | bytes 3080 | tf_op jit(solution)/shard_map/ppermute | solution.py:14
  30.0 5.6 %collective-permute-start.7 = (f32[256]{0:T(256)S(1)}, f32[256]{0:T(256)S(1)}, u32[]{:S(2)}, u32[]{:S(2)}) collective-permute-start(f32[256]{0:T(256)S(1)} %bitcast.267), channel_id=1, source_target_pairs={{0,1},{1,2},{2,3},{3,4},{4,5},{5,6},{6,7},{7,8},{8,9},{9,10},{10,1... | collective-permute-start | bytes 3080 | tf_op jit(solution)/shard_map/ppermute | solution.py:14
  39.8 4.9 %collective-permute-start.8 = (f32[256]{0:T(256)S(1)}, f32[256]{0:T(256)S(1)}, u32[]{:S(2)}, u32[]{:S(2)}) collective-permute-start(f32[256]{0:T(256)S(1)} %add.178), channel_id=1, source_target_pairs={{1,0},{2,1},{3,2},{4,3},{5,4},{6,5},{7,6},{8,7},{9,8},{10,9},{11,1... | collective-permute-start | bytes 3080 | tf_op jit(solution)/shard_map/ppermute | solution.py:14
  41.6 3.9 %collective-permute-start.9 = (f32[256]{0:T(256)S(1)}, f32[256]{0:T(256)S(1)}, u32[]{:S(2)}, u32[]{:S(2)}) collective-permute-start(f32[256]{0:T(256)S(1)} %bitcast.269), channel_id=1, source_target_pairs={{0,1},{1,2},{2,3},{3,4},{4,5},{5,6},{6,7},{7,8},{8,9},{9,10},{10,1... | collective-permute-start | bytes 3080 | tf_op jit(solution)/shard_map/ppermute | solution.py:14
  46.1 59.9 %collective-permute-start.10 = (f32[256]{0:T(256)S(1)}, f32[256]{0:T(256)S(1)}, u32[]{:S(2)}, u32[]{:S(2)}) collective-permute-start(f32[256]{0:T(256)S(1)} %get-tuple-element.41), channel_id=1, source_target_pairs={{1,0},{2,1},{3,2},{4,3},{5,4},{6,5},{7,6},{8,7},{9,8},{10,9},{11,1... | collective-permute-start | bytes 3080 | tf_op jit(solution)/shard_map/ppermute | solution.py:14
  47.9 58.4 %collective-permute-start.11 = (f32[256]{0:T(256)S(1)}, f32[256]{0:T(256)S(1)}, u32[]{:S(2)}, u32[]{:S(2)}) collective-permute-start(f32[256]{0:T(256)S(1)} %bitcast.259), channel_id=1, source_target_pairs={{0,1},{1,2},{2,3},{3,4},{4,5},{5,6},{6,7},{7,8},{8,9},{9,10},{10,1... | collective-permute-start | bytes 3080 | tf_op jit(solution)/shard_map/ppermute | solution.py:14
  107.0 51.3 %collective-permute-start.12 = (f32[256]{0:T(256)S(1)}, f32[256]{0:T(256)S(1)}, u32[]{:S(2)}, u32[]{:S(2)}) collective-permute-start(f32[256]{0:T(256)S(1)} %mul.220), channel_id=1, source_target_pairs={{1,0},{2,1},{3,2},{4,3},{5,4},{6,5},{7,6},{8,7},{9,8},{10,9},{11,1... | collective-permute-start | bytes 3080 | tf_op jit(solution)/shard_map/ppermute | solution.py:14
  152.9 5.7 %collective-permute-start.13 = (f32[256]{0:T(256)S(1)}, f32[256]{0:T(256)S(1)}, u32[]{:S(2)}, u32[]{:S(2)}) collective-permute-start(f32[256]{0:T(256)S(1)} %bitcast.257), channel_id=1, source_target_pairs={{0,1},{1,2},{2,3},{3,4},{4,5},{5,6},{6,7},{7,8},{8,9},{9,10},{10,1... | collective-permute-start | bytes 3080 | tf_op jit(solution)/shard_map/ppermute | solution.py:14
  161.1 4.9 %collective-permute-start.14 = (f32[256]{0:T(256)S(1)}, f32[256]{0:T(256)S(1)}, u32[]{:S(2)}, u32[]{:S(2)}) collective-permute-start(f32[256]{0:T(256)S(1)} %add.190), channel_id=1, source_target_pairs={{1,0},{2,1},{3,2},{4,3},{5,4},{6,5},{7,6},{8,7},{9,8},{10,9},{11,1... | collective-permute-start | bytes 3080 | tf_op jit(solution)/shard_map/ppermute | solution.py:14
  162.9 3.9 %collective-permute-start.15 = (f32[256]{0:T(256)S(1)}, f32[256]{0:T(256)S(1)}, u32[]{:S(2)}, u32[]{:S(2)}) collective-permute-start(f32[256]{0:T(256)S(1)} %bitcast.271), channel_id=1, source_target_pairs={{0,1},{1,2},{2,3},{3,4},{4,5},{5,6},{6,7},{7,8},{8,9},{9,10},{10,1... | collective-permute-start | bytes 3080 | tf_op jit(solution)/shard_map/ppermute | solution.py:14
  166.8 5.7 %collective-permute-start.16 = (f32[256]{0:T(256)S(1)}, f32[256]{0:T(256)S(1)}, u32[]{:S(2)}, u32[]{:S(2)}) collective-permute-start(f32[256]{0:T(256)S(1)} %multiply_add_fusion.1), channel_id=1, source_target_pairs={{1,0},{2,1},{3,2},{4,3},{5,4},{6,5},{7,6},{8,7},{9,8},{10,9},{11,1... | collective-permute-start | bytes 3080 | tf_op jit(solution)/shard_map/ppermute | solution.py:14
  168.6 4.7 %collective-permute-start.17 = (f32[256]{0:T(256)S(1)}, f32[256]{0:T(256)S(1)}, u32[]{:S(2)}, u32[]{:S(2)}) collective-permute-start(f32[256]{0:T(256)S(1)} %bitcast.261), channel_id=1, source_target_pairs={{0,1},{1,2},{2,3},{3,4},{4,5},{5,6},{6,7},{7,8},{8,9},{9,10},{10,1... | collective-permute-start | bytes 3080 | tf_op jit(solution)/shard_map/ppermute | solution.py:14
